TPU v7x, 32 devices: a whole 2x2x4 slice. The times are simulated.
32 devices in a mesh: tm: 4 (over y, x), sx: 2 (over core), sy: 4 (over z).
Axes of the slice: x: 2, y: 2, z: 4, core: 2. Of those that a mesh axis runs over, the one named last changes fastest.
Arguments:
- iterate: float32 [32, 512, 1024], P('tm', 'sx', 'sy'), may hold values from -6 to 6
- source: float32 [32, 512, 1024], P('tm', 'sx', 'sy'), may hold values from -6 to 6
- start_field: float32 [512, 1024], P('sx', 'sy'), may hold values from -6 to 6
- conduct: float32 [512, 1024], P('sx', 'sy'), may hold values from 0.2 to 5
Outputs:
- updated: float32 [32, 512, 1024], P('tm', 'sx', 'sy')
- coarse_residual: float32 [8, 512, 1024], P('tm', 'sx', 'sy')
All inputs are finite; a program needn't handle non-finite values.
Results may differ from a plain program's by a relative error of at most 0.00002.
Values sent between devices are 32-bit elements; how exact they have to be, the bound alone decides.
A program may use at most 128 MiB of HBM per device.

v0:
```python
import functools
import jax
import jax.numpy as jnp
from jax import lax
from jax.experimental import pallas as pl
from jax.experimental.pallas import tpu as pltpu
from jax.sharding import PartitionSpec as P

FACTOR = 4
SWEEPS = 2
LANES = 128
PAD = 8
STRIP = 32
MESH = pl.DeviceIdType.MESH


def round_up(value, unit):
    return -(-value // unit) * unit


def when_all(*conds):
    total = conds[0]
    for cond in conds[1:]:
        total = jnp.logical_and(total, cond)
    return pl.when(total)


def kernel(
    sizes, rows, cols, count,
    iterate_ref, source_ref, start_ref, conduct_ref,
    out_ref, resid_ref,
    fields, inv, gain, rhs, half, points,
    pack_right, pack_left, from_left, from_right,
    rc, errors, cinv, cgain, chalf,
    cpack_right, cpack_left, cfrom_left, cfrom_right,
    out_v, resid_v, folded,
    local_sems, up_sems, side_sems, time_sems, rc_send, rc_recv, out_sems,
):
    nt, nx, ny = sizes
    t, x, y = lax.axis_index("tm"), lax.axis_index("sx"), lax.axis_index("sy")
    f32 = jnp.float32
    halo = 2 * SWEEPS * FACTOR
    planes = cols // LANES
    top = PAD + halo
    ext = rows + 2 * halo
    levels = nt * count
    crows, cplanes = rows // 2, cols // 2 // LANES
    chalo = (rc.shape[2] - 2 * PAD - crows) // 2
    ctop = PAD + chalo
    cext = crows + 2 * chalo
    per_interval = FACTOR + 1
    n_first = 1 + per_interval * (count - 1)

    def base_of(k):
        return 1 + per_interval * (count - 1 - k) - (k == 0)

    def start_of(k):
        return base_of(k) if k > 0 else n_first + FACTOR

    def zero_rows(ref, start, size):
        ref[..., pl.ds(start, size), :] = jnp.zeros(ref.shape[:-2] + (size, LANES), f32)

    def zero_halos(i, carry):
        for p in range(planes):
            fields[i, p, pl.ds(PAD, halo), :] = jnp.zeros((halo, LANES), f32)
            fields[i, p, pl.ds(top + rows, halo), :] = jnp.zeros((halo, LANES), f32)
        return carry

    lax.fori_loop(0, fields.shape[0], zero_halos, 0)

    def zero_leading(ref):
        n = ref.shape[-2]

        def body(i, carry):
            ref[i] = jnp.zeros(ref.shape[1:], f32)
            return carry

        lax.fori_loop(0, ref.shape[0], body, 0)

    for ref in (from_left, from_right, cfrom_left, cfrom_right, rc, folded):
        zero_leading(ref)
    loads = []

    def load(src, field, sem):
        for p in range(planes):
            copy = pltpu.make_async_copy(
                src.at[:, pl.ds(p * LANES, LANES)],
                fields.at[field, p, pl.ds(top, rows), :],
                local_sems.at[sem + p],
            )
            copy.start()
            loads.append(copy)

    sem = 0
    load(conduct_ref, 0, sem)
    sem += planes
    for k in range(count - 1, -1, -1):
        if k > 0:
            load(iterate_ref.at[k * FACTOR - 1], start_of(k), sem)
            sem += planes
        for j in range(FACTOR):
            load(source_ref.at[k * FACTOR + j], base_of(k) + 1 + j, sem)
            sem += planes
    first_loads = len(loads) - planes * FACTOR
    opening = [
        pltpu.make_async_copy(
            start_ref.at[:, pl.ds(p * LANES, LANES)],
            fields.at[start_of(0), p, pl.ds(top, rows), :],
            local_sems.at[sem + p],
        )
        for p in range(planes)
    ]

    @pl.when(t == 0)
    def _():
        for copy in opening:
            copy.start()

    barrier = pltpu.get_barrier_semaphore()
    has_up, has_down = x > 0, x < nx - 1
    has_left, has_right = y > 0, y < ny - 1
    has_prev, has_next = t > 0, t < nt - 1
    arrivals = jnp.int32(nt - 1)
    for cond, target in (
        (has_up, {"sx": x - 1}), (has_down, {"sx": x + 1}),
        (has_left, {"sy": y - 1}), (has_right, {"sy": y + 1}),
    ):
        arrivals += jnp.where(cond, 1, 0)

        @pl.when(cond)
        def _(target=target):
            pl.semaphore_signal(barrier, inc=1, device_id=target, device_id_type=MESH)

    for other in range(nt):
        @pl.when(t != other)
        def _(other=other):
            pl.semaphore_signal(barrier, inc=1, device_id={"tm": other}, device_id_type=MESH)

    pl.semaphore_wait(barrier, arrivals)

    def remote(src, dst, sems, number, target):
        return pltpu.make_async_remote_copy(
            src_ref=src, dst_ref=dst, send_sem=sems.at[0, number], recv_sem=sems.at[1, number],
            device_id=target, device_id_type=MESH,
        )

    old = [
        remote(
            iterate_ref.at[count * FACTOR - 1, :, pl.ds(p * LANES, LANES)],
            fields.at[start_of(0), p, pl.ds(top, rows), :],
            time_sems, p, {"tm": t + 1},
        )
        for p in range(planes)
    ]

    @pl.when(has_next)
    def _():
        for copy in old:
            copy.start()

    lane = lax.broadcasted_iota(jnp.int32, (8, LANES), 1)

    def row_exchange(ref, lead, width, own_top, own_rows, depth, sems, number):
        def part(start):
            return ref.at[lead, pl.ds(0, width), pl.ds(start, depth), :]

        down = remote(part(own_top + own_rows - depth), part(own_top - depth), sems, number, {"sx": x + 1})
        up = remote(part(own_top), part(own_top + own_rows), sems, number + 1, {"sx": x - 1})

        @pl.when(has_down)
        def _():
            down.start()

        @pl.when(has_up)
        def _():
            up.start()

        @pl.when(has_up)
        def _():
            down.wait_recv()

        @pl.when(has_down)
        def _():
            up.wait_recv()

        @pl.when(has_down)
        def _():
            down.wait_send()

        @pl.when(has_up)
        def _():
            up.wait_send()

    def side_exchange(ref, first, slots, width, depth, length, right, left, in_left, in_right, tile0, sems, number):
        per_tile = LANES // depth
        tiles = -(-slots // per_tile)
        chunk = 32
        for tile in range(tiles):
            members = range(tile * per_tile, min(slots, (tile + 1) * per_tile))
            wide = lax.broadcasted_iota(jnp.int32, (chunk, LANES), 1)

            def pack(i, carry, members=members, tile=tile):
                at = pl.ds(PAD + i * chunk, chunk)
                to_right = to_left = jnp.zeros((chunk, LANES), f32)
                for place, slot in enumerate(members):
                    here = jnp.logical_and(wide >= place * depth, wide < (place + 1) * depth)
                    last, head = ref[first + slot, width - 1, at, :], ref[first + slot, 0, at, :]
                    to_right = jnp.where(here, pltpu.roll(last, (place * depth + depth) % LANES, 1), to_right)
                    to_left = jnp.where(here, pltpu.roll(head, place * depth, 1), to_left)
                right[tile0 + tile, pl.ds(i * chunk, chunk), :] = to_right
                left[tile0 + tile, pl.ds(i * chunk, chunk), :] = to_left
                return carry

            lax.fori_loop(0, length // chunk, pack, 0)
        span = pl.ds(tile0, tiles)
        go_right = remote(right.at[span], in_left.at[span], sems, number, {"sy": y + 1})
        go_left = remote(left.at[span], in_right.at[span], sems, number + 1, {"sy": y - 1})

        @pl.when(has_right)
        def _():
            go_right.start()

        @pl.when(has_left)
        def _():
            go_left.start()

        def finish():
            @pl.when(has_left)
            def _():
                go_right.wait_recv()

            @pl.when(has_right)
            def _():
                go_left.wait_recv()

            for tile in range(tiles):
                members = range(tile * per_tile, min(slots, (tile + 1) * per_tile))
                wide = lax.broadcasted_iota(jnp.int32, (chunk, LANES), 1)

                def unpack(i, carry, members=members, tile=tile):
                    at = pl.ds(PAD + i * chunk, chunk)
                    came_right = in_right[tile0 + tile, pl.ds(i * chunk, chunk), :]
                    came_left = in_left[tile0 + tile, pl.ds(i * chunk, chunk), :]
                    for place, slot in enumerate(members):
                        on_right = pltpu.roll(came_right, (-place * depth) % LANES, 1)
                        on_left = pltpu.roll(came_left, (LANES - depth - place * depth) % LANES, 1)
                        ref[first + slot, width, at, :] = jnp.where(
                            wide < depth, on_right, jnp.where(wide >= LANES - depth, on_left, 0.0)
                        )
                    return carry

                lax.fori_loop(0, length // chunk, unpack, 0)

            @pl.when(has_right)
            def _():
                go_right.wait_send()

            @pl.when(has_left)
            def _():
                go_left.wait_send()

        return finish

    groups = LANES // (2 * halo)
    seg = ext // groups

    def fold(plane, dst):
        wide = lax.broadcasted_iota(jnp.int32, (seg, LANES), 1)
        total = jnp.zeros((seg, LANES), f32)
        for g in range(groups):
            part = pltpu.roll(plane[pl.ds(PAD + g * seg, seg), :], (halo + 2 * halo * g) % LANES, 1)
            total = jnp.where(wide // (2 * halo) == g, part, total)
        dst[...] = total

    def unfold(on_right, on_left, plane):
        wide = lax.broadcasted_iota(jnp.int32, (seg, LANES), 1)
        for g in range(groups):
            back = (-(halo + 2 * halo * g)) % LANES
            plane[pl.ds(PAD + g * seg, seg), :] = jnp.where(
                wide < halo, pltpu.roll(on_right[...], back, 1),
                jnp.where(wide >= LANES - halo, pltpu.roll(on_left[...], back, 1), 0.0),
            )

    def strips(length, body, lead=0):
        for start in range(0, length, STRIP):
            body(lead + start, min(STRIP, length - start))

    def total_of(ref, width, at, size):
        wide = lax.broadcasted_iota(jnp.int32, (size, LANES), 1)
        ahead, behind = [], []
        for p in range(width):
            own = ref[p, pl.ds(at, size), :]
            behind.append(pltpu.roll(own, 1, 1))
            ahead.append(pltpu.roll(own, LANES - 1, 1))
        result = []
        for p in range(width):
            vert = ref[p, pl.ds(at + 1, size), :] + ref[p, pl.ds(at - 1, size), :]
            nxt = jnp.where(wide == LANES - 1, ahead[(p + 1) % width], ahead[p])
            prv = jnp.where(wide == 0, behind[(p - 1) % width], behind[p])
            result.append(vert + (nxt + prv))
        return result

    def sweep(src, b, ivs, gs, width, length, emit, lead):
        def body(offset, size):
            at = PAD + offset
            sums = total_of(src, width, at, size)
            for p in range(width):
                rows_at = pl.ds(at, size)
                emit(p, offset, size, b[p, rows_at, :] * ivs[p, rows_at, :] + gs[p, rows_at, :] * sums[p])

        strips(length, body, lead)

    def phi(b, emit, ivs=inv, gs=gain, mid=half, width=planes + 1, length=ext, lead=0):
        def keep(p, offset, size, value):
            mid[p, pl.ds(PAD + offset, size), :] = value

        sweep(b, b, ivs, gs, width, length, keep, lead)
        sweep(mid, b, ivs, gs, width, length, emit, lead)

    def fill(value):
        def body(offset, size):
            at = pl.ds(PAD + offset, size)
            for p in range(planes + 1):
                rhs[p, at, :] = value(p, at)

        strips(ext, body)

    def first_pass(k):
        base = base_of(k)
        fill(lambda p, at: fields[start_of(k), p, at, :] + fields[base + 1, p, at, :])

        def one(j, carry):
            def emit(p, offset, size, value):
                at = pl.ds(PAD + offset, size)
                rhs[p, at, :] = value + fields[base + 2 + j, p, at, :]

            phi(rhs, emit)
            return carry

        lax.fori_loop(0, FACTOR - 1, one, 0)

        def last(p, offset, size, value):
            points[k + 1, p, pl.ds(PAD + offset, size), :] = value

        phi(rhs, last)

    def coefficients(src, ivs, gs, width, length):
        def body(offset, size):
            at = pl.ds(PAD + offset, size)
            for p in range(width):
                c = src[p, at, :]
                one = 1.0 / (1.0 + 4.0 * c)
                ivs[p, at, :] = one
                gs[p, at, :] = c * one

        strips(length, body)

    lane_in = lax.broadcasted_iota(jnp.int32, (LANES, LANES), 0)
    lane_out = lax.broadcasted_iota(jnp.int32, (LANES, LANES), 1)

    def dot(a, b):
        return jnp.dot(a, b, precision=lax.Precision.HIGHEST, preferred_element_type=f32)

    def restrict(ref, own_top, store):
        pairs = []
        for p in range(planes):
            pairs.append(ref[p, pl.ds(own_top, crows, stride=2), :] + ref[p, pl.ds(own_top + 1, crows, stride=2), :])
        for q in range(cplanes):
            value = jnp.zeros((crows, LANES), f32)
            for side in range(2):
                pick = jnp.where(lane_in // 2 + side * (LANES // 2) == lane_out, 0.25, 0.0)
                value += dot(pairs[2 * q + side], pick)
            store(q, value)

    for copy in loads[:first_loads]:
        copy.wait()

    def keep_coarse(q, value):
        rc[0, q, pl.ds(ctop, crows), :] = value

    first_tiles = -(-n_first // (LANES // halo))
    row_exchange(fields, pl.ds(0, n_first), planes, top, rows, halo, up_sems, 0)
    finish = side_exchange(
        fields, 0, n_first, planes, halo, ext, pack_right, pack_left, from_left, from_right, 0, side_sems, 0
    )
    for copy in loads[first_loads:]:
        copy.wait()
    row_exchange(fields, pl.ds(n_first, FACTOR), planes, top, rows, halo, up_sems, 2)
    finish_sources = side_exchange(
        fields, n_first, FACTOR, planes, halo, ext,
        pack_right, pack_left, from_left, from_right, first_tiles, side_sems, 2,
    )
    for ref in (rhs, half, chalf):
        zero_rows(ref, 0, PAD)
        zero_rows(ref, ref.shape[-2] - PAD, PAD)
    zero_leading(errors)
    for start in (PAD, top + rows + halo // 2):
        points[0, :, pl.ds(start, halo // 2), :] = jnp.zeros((planes + 1, halo // 2, LANES), f32)
    restrict(fields.at[0], top, keep_coarse)
    finish()
    coefficients(fields.at[0], inv, gain, planes + 1, ext)
    near = pl.ds(top - halo // 2, rows + halo)
    for k in range(count - 1, 0, -1):
        first_pass(k)
        if k == count - 1:
            fold(points.at[count, planes], folded.at[0])
            sent = [
                remote(points.at[count, pl.ds(0, planes), near, :], points.at[0, pl.ds(0, planes), near, :], time_sems, planes, {"tm": t + 1}),
                remote(folded.at[0], folded.at[1], time_sems, planes + 1, {"tm": t + 1}),
            ]

            @pl.when(has_next)
            def _():
                for copy in sent:
                    copy.start()

    @pl.when(t == 0)
    def _():
        for copy in opening:
            copy.wait()

    @pl.when(has_prev)
    def _():
        for copy in old:
            copy.wait_recv()

    last_field = n_first + FACTOR
    row_exchange(fields, pl.ds(last_field, 1), planes, top, rows, halo, up_sems, 6)
    fold(fields.at[last_field, planes - 1], folded.at[2])
    fold(fields.at[last_field, 0], folded.at[3])
    go_right = remote(folded.at[2], folded.at[4], side_sems, 6, {"sy": y + 1})
    go_left = remote(folded.at[3], folded.at[5], side_sems, 7, {"sy": y - 1})

    @pl.when(has_right)
    def _():
        go_right.start()

    @pl.when(has_left)
    def _():
        go_left.start()

    finish_sources()

    @pl.when(has_left)
    def _():
        go_right.wait_recv()

    @pl.when(has_right)
    def _():
        go_left.wait_recv()

    unfold(folded.at[5], folded.at[4], fields.at[last_field, planes])

    @pl.when(has_right)
    def _():
        go_right.wait_send()

    @pl.when(has_left)
    def _():
        go_left.wait_send()

    first_pass(0)

    trim = dict(length=rows + halo, lead=halo // 2)
    stores = []

    def put(src, dst, number):
        copy = pltpu.make_async_copy(src, dst, out_sems.at[number])
        copy.start()
        stores.append(copy)

    def level_of(block, k):
        return rc.at[pl.ds(1 + block * count + k, 1), pl.ds(0, cplanes), pl.ds(ctop, crows), :]

    def level_copy(block, k, other):
        return pltpu.make_async_remote_copy(
            src_ref=level_of(block, k), dst_ref=level_of(block, k),
            send_sem=rc_send.at[other, k], recv_sem=rc_recv.at[block, k],
            device_id={"tm": other}, device_id_type=MESH,
        )

    def residual(k):
        fill(lambda p, at: points[k, p, at, :] - fields[start_of(k), p, at, :])

        def one(j, carry):
            def emit(p, offset, size, value):
                rhs[p, pl.ds(PAD + offset, size), :] = value

            phi(rhs, emit, **trim)
            return carry

        lax.fori_loop(0, FACTOR, one, 0)

        def store(q, value):
            rc[1 + t * count + k, q, pl.ds(ctop, crows), :] = value

        restrict(rhs, top, store)
        for other in range(1, nt):
            copy = level_copy(t, k, other)

            @pl.when(t < other)
            def _(copy=copy):
                copy.start()

        for p in range(planes):
            resid_v[k, :, pl.ds(p * LANES, LANES)] = rhs[p, pl.ds(top, rows), :]
        put(resid_v.at[k], resid_ref.at[k], count * FACTOR + k)

    for k in range(count - 1, 0, -1):
        residual(k)

    @pl.when(t == 0)
    def _():
        for p in range(planes + 1):
            points[0, p, near, :] = fields[start_of(0), p, near, :]

    @pl.when(has_prev)
    def _():
        for copy in sent:
            copy.wait_recv()
        unfold(folded.at[1], folded.at[1], points.at[0, planes])

    residual(0)

    for other in range(nt - 1):
        @pl.when(t > other)
        def _(other=other):
            for k in range(count):
                level_copy(other, k, other).wait_recv()

    for other in range(1, nt):
        @pl.when(t < other)
        def _(other=other):
            for k in range(count):
                level_copy(t, k, other).wait_send()

    row_exchange(rc, pl.ds(0, levels), cplanes, ctop, crows, chalo, up_sems, 4)
    finish = side_exchange(
        rc, 0, levels, cplanes, chalo, cext,
        cpack_right, cpack_left, cfrom_left, cfrom_right, 0, side_sems, 4,
    )
    finish()
    coefficients(rc.at[0], cinv, cgain, cplanes + 1, cext)

    def level(n, carry):
        def emit(p, offset, size, value):
            at = pl.ds(PAD + offset, size)
            errors[n + 1, p, at, :] = value + rc[n + 1, p, at, :]

        phi(errors.at[n], emit, cinv, cgain, chalf, cplanes + 1, cext)
        return carry

    lax.fori_loop(0, levels, level, 0)

    picks = []
    for p in range(planes):
        picks.append(jnp.where(lane_in == lane_out // 2 + (p % 2) * (LANES // 2), 1.0, 0.0))
    rim = jnp.where(lane_out < LANES // 2, lane_out // 2, LANES // 2 + lane_out // 2)
    picks.append(jnp.where(lane_in == rim, 1.0, 0.0))
    span = ext // 2
    shift = ctop - halo // 2

    def correct(k):
        for p in range(planes + 1):
            plane = errors[t * count + k, cplanes if p == planes else p // 2, pl.ds(shift, span), :]
            wide = dot(plane, picks[p])
            for odd in range(2):
                half[p, pl.ds(PAD + odd, span, stride=2), :] = wide

        def body(offset, size):
            at = pl.ds(PAD + offset, size)
            for p in range(planes + 1):
                points[k, p, at, :] = points[k, p, at, :] + half[p, at, :]

        strips(rows + halo, body, halo // 2)

    @pl.when(has_next)
    def _():
        for copy in sent + old:
            copy.wait_send()

    for k in range(count + 1):
        correct(k)
        if k > 0:
            for p in range(planes):
                out_v[k * FACTOR - 1, :, pl.ds(p * LANES, LANES)] = points[k, p, pl.ds(top, rows), :]
            put(out_v.at[k * FACTOR - 1], out_ref.at[k * FACTOR - 1], k * FACTOR - 1)

    for k in range(count):
        base = base_of(k)
        fill(lambda p, at: points[k, p, at, :] + fields[base + 1, p, at, :])
        for j in range(FACTOR - 1):
            def emit(p, offset, size, value, j=j):
                at = pl.ds(PAD + offset, size)
                if j < FACTOR - 2:
                    rhs[p, at, :] = value + fields[base + 2 + j, p, at, :]
                low, high = max(offset, halo), min(offset + size, halo + rows)
                if p < planes and low < high:
                    own = value[low - offset : high - offset]
                    out_v[k * FACTOR + j, pl.ds(low - halo, high - low), pl.ds(p * LANES, LANES)] = own

            phi(rhs, emit, **trim)
            put(out_v.at[k * FACTOR + j], out_ref.at[k * FACTOR + j], k * FACTOR + j)

    for copy in stores:
        copy.wait()


def solution(mesh):
    sizes = tuple(mesh.shape[name] for name in ("tm", "sx", "sy"))

    def shards(iterate, source, start_field, conduct):
        steps, rows, cols = iterate.shape
        count = steps // FACTOR
        levels = sizes[0] * count
        halo = 2 * SWEEPS * FACTOR
        planes, cplanes = cols // LANES, cols // 2 // LANES
        tall = rows + 2 * halo + 2 * PAD
        chalo = round_up(SWEEPS * levels, 16)
        ctall = rows // 2 + 2 * chalo + 2 * PAD
        n_fields = 1 + (FACTOR + 1) * count
        per_tile = LANES // halo
        tiles = -(-(n_fields - FACTOR - 1) // per_tile) + 1
        ctiles = -(-levels // (LANES // chalo))
        f32 = jnp.float32
        field = pltpu.VMEM((planes + 1, tall, LANES), f32)
        packed = pltpu.VMEM((tiles, rows + 2 * halo, LANES), f32)
        cfield = pltpu.VMEM((cplanes + 1, ctall, LANES), f32)
        cpacked = pltpu.VMEM((ctiles, rows // 2 + 2 * chalo, LANES), f32)
        n_loads = planes * (n_fields + 1)
        dma = pltpu.SemaphoreType.DMA
        return pl.pallas_call(
            functools.partial(kernel, sizes, rows, cols, count),
            out_shape=(
                jax.ShapeDtypeStruct((steps, rows, cols), f32),
                jax.ShapeDtypeStruct((count, rows, cols), f32),
            ),
            in_specs=[pl.BlockSpec(memory_space=pltpu.MemorySpace.HBM)] * 4,
            out_specs=[pl.BlockSpec(memory_space=pltpu.MemorySpace.HBM)] * 2,
            scratch_shapes=[
                pltpu.VMEM((n_fields, planes + 1, tall, LANES), f32),
                field, field, field, field,
                pltpu.VMEM((count + 1, planes + 1, tall, LANES), f32),
                packed, packed, packed, packed,
                pltpu.VMEM((levels + 1, cplanes + 1, ctall, LANES), f32),
                pltpu.VMEM((levels + 1, cplanes + 1, ctall, LANES), f32),
                cfield, cfield, cfield,
                cpacked, cpacked, cpacked, cpacked,
                pltpu.VMEM((steps, rows, cols), f32),
                pltpu.VMEM((count, rows, cols), f32),
                pltpu.VMEM((6, (rows + 2 * halo) // (LANES // (2 * halo)), LANES), f32),
                dma((n_loads,)), dma((2, 8)), dma((2, 8)), dma((2, planes + 2)),
                dma((sizes[0], count)), dma((sizes[0], count)), dma((steps + count,)),
            ],
            compiler_params=pltpu.CompilerParams(
                collective_id=0, has_side_effects=True, vmem_limit_bytes=60 * 1024 * 1024
            ),
        )(iterate, source, start_field, conduct)

    in_specs = (P("tm", "sx", "sy"), P("tm", "sx", "sy"), P("sx", "sy"), P("sx", "sy"))
    out_specs = (P("tm", "sx", "sy"), P("tm", "sx", "sy"))
    return jax.shard_map(shards, mesh=mesh, in_specs=in_specs, out_specs=out_specs, check_vma=False)
```

profile of v0, /device:TPU:0, one launch (start us, length us, event | category | flops | bytes accessed | tf_op | source)
XLA Modules:
  0.0 49.0 jit_solution(249977443252191636)
XLA Ops:
  0.6 44.5 %shard_map.59 = (f32[8,256,256]{2,1,0:T(8,128)}, f32[2,256,256]{2,1,0:T(8,128)}) custom-call(f32[8,256,256]{2,1,0:T(8,128)} %iterate_ref.1, f32[8,256,256]{2,1,0:T(8,128)} %source_ref.1, f32[256,256]{1,0:T(8,128)} %start_ref.1, f32[256,256]{1,0:T(8,128)} %conduct_ref.1), custom_call_target="tpu_custom_call" | custom-call | tf_op jit(solution)/shard_map/pallas_call | solution.py:632
  45.1 0.0 copy-start
  45.1 3.1 %copy.8 = f32[8,256,256]{2,1,0:T(8,128)} copy(f32[8,256,256]{2,1,0:T(8,128)} %get-tuple-element.4) | data formatting | bytes 4194304
  48.2 0.0 copy-done
  48.2 0.8 %copy.9 = f32[2,256,256]{2,1,0:T(8,128)} copy(f32[2,256,256]{2,1,0:T(8,128)S(1)} %copy-done) | data formatting | bytes 1048576
Async XLA Ops:
  45.1 3.1 %copy-start = (f32[2,256,256]{2,1,0:T(8,128)S(1)}, f32[2,256,256]{2,1,0:T(8,128)}, u32[]{:S(2)}) copy-start(f32[2,256,256]{2,1,0:T(8,128)} %get-tuple-element.5) | copy-start | bytes 1572868
where the time goes:
time: 49.2 us; the launch traced here: 49 us
  Pallas kernels  44.5 us (90%)
  local copies, waits for them, and re-layouts  3.9 us (8%)
  between operations  0.65 us (1%)
    pallas_call x1, Pallas kernels, shards(): pl.pallas_call(functools.partial(kernel, sizes, rows, cols, count), out_s...  44.5 us
    unnamed x4, local copies, waits for them, and re-layouts  3.9 us

commit v1 on v0

--- a/solution.py
+++ b/solution.py
@@ -33,12 +33,13 @@
     pack_right, pack_left, from_left, from_right,
     rc, errors, cinv, cgain, chalf,
     cpack_right, cpack_left, cfrom_left, cfrom_right,
-    out_v, resid_v, folded,
+    folded,
     local_sems, up_sems, side_sems, time_sems, rc_send, rc_recv, out_sems,
 ):
     nt, nx, ny = sizes
     t, x, y = lax.axis_index("tm"), lax.axis_index("sx"), lax.axis_index("sy")
     f32 = jnp.float32
+    out_v, resid_v = out_ref, resid_ref
     halo = 2 * SWEEPS * FACTOR
     planes = cols // LANES
     top = PAD + halo
@@ -465,9 +466,7 @@
     stores = []
 
     def put(src, dst, number):
-        copy = pltpu.make_async_copy(src, dst, out_sems.at[number])
-        copy.start()
-        stores.append(copy)
+        pass
 
     def level_of(block, k):
         return rc.at[pl.ds(1 + block * count + k, 1), pl.ds(0, cplanes), pl.ds(ctop, crows), :]
@@ -629,14 +628,14 @@
         cpacked = pltpu.VMEM((ctiles, rows // 2 + 2 * chalo, LANES), f32)
         n_loads = planes * (n_fields + 1)
         dma = pltpu.SemaphoreType.DMA
-        return pl.pallas_call(
+        res = pl.pallas_call(
             functools.partial(kernel, sizes, rows, cols, count),
             out_shape=(
-                jax.ShapeDtypeStruct((steps, rows, cols), f32),
-                jax.ShapeDtypeStruct((count, rows, cols), f32),
+                pltpu.VMEM((steps, rows, cols), f32),
+                pltpu.VMEM((count, rows, cols), f32),
             ),
             in_specs=[pl.BlockSpec(memory_space=pltpu.MemorySpace.HBM)] * 4,
-            out_specs=[pl.BlockSpec(memory_space=pltpu.MemorySpace.HBM)] * 2,
+            out_specs=[pl.BlockSpec(memory_space=pltpu.MemorySpace.VMEM)] * 2,
             scratch_shapes=[
                 pltpu.VMEM((n_fields, planes + 1, tall, LANES), f32),
                 field, field, field, field,
@@ -646,16 +645,31 @@
                 pltpu.VMEM((levels + 1, cplanes + 1, ctall, LANES), f32),
                 cfield, cfield, cfield,
                 cpacked, cpacked, cpacked, cpacked,
-                pltpu.VMEM((steps, rows, cols), f32),
-                pltpu.VMEM((count, rows, cols), f32),
                 pltpu.VMEM((6, (rows + 2 * halo) // (LANES // (2 * halo)), LANES), f32),
                 dma((n_loads,)), dma((2, 8)), dma((2, 8)), dma((2, planes + 2)),
                 dma((sizes[0], count)), dma((sizes[0], count)), dma((steps + count,)),
             ],
             compiler_params=pltpu.CompilerParams(
-                collective_id=0, has_side_effects=True, vmem_limit_bytes=60 * 1024 * 1024
+                collective_id=0, has_side_effects=True, vmem_limit_bytes=48 * 1024 * 1024
             ),
-        )(iterate, source, start_field, conduct)
+        )(*[pltpu.with_memory_space_constraint(z, pltpu.MemorySpace.HBM) for z in (iterate, source, start_field, conduct)])
+
+        def put(a, b, oa, ob, sems):
+            n = a.shape[0]
+            cs = [pltpu.make_async_copy(a.at[i], oa.at[i], sems.at[i]) for i in range(n)]
+            cs += [pltpu.make_async_copy(b.at[i], ob.at[i], sems.at[n + i]) for i in range(b.shape[0])]
+            for c in cs:
+                c.start()
+            for c in cs:
+                c.wait()
+
+        return pl.pallas_call(
+            put,
+            out_shape=(jax.ShapeDtypeStruct((steps, rows, cols), f32), jax.ShapeDtypeStruct((count, rows, cols), f32)),
+            in_specs=[pl.BlockSpec(memory_space=pltpu.MemorySpace.VMEM)] * 2,
+            out_specs=[pl.BlockSpec(memory_space=pltpu.MemorySpace.HBM)] * 2,
+            scratch_shapes=[dma((steps + count,))],
+        )(*[pltpu.with_memory_space_constraint(z, pltpu.MemorySpace.VMEM) for z in res])
 
     in_specs = (P("tm", "sx", "sy"), P("tm", "sx", "sy"), P("sx", "sy"), P("sx", "sy"))
     out_specs = (P("tm", "sx", "sy"), P("tm", "sx", "sy"))

time: 49.2 us -> 46.2 us (0.939)
  local copies, waits for them, and re-layouts: 3.9 us -> 0 us
  Pallas kernels: 44.5 us -> 45.4 us
    unnamed x4 -> x0, local copies, waits for them, and re-layouts: 3.9 us -> none
    pallas_call x0 -> x1, Pallas kernels: none -> 1.57 us  [shards(): pl.pallas_call(put, out_shape=(jax.ShapeDtypeStruct((steps, rows, cols),...]
    pallas_call x1, Pallas kernels: 44.5 us -> 43.8 us  [shards(): pl.pallas_call(functools.partial(kernel, sizes, rows, cols, count), out_s...]
where the time goes in v1:
time: 46.2 us; the launch traced here: 46 us
  Pallas kernels  45.4 us (98%)
  between operations  0.64 us (1%)
    pallas_call x1, Pallas kernels, shards(): pl.pallas_call(functools.partial(kernel, sizes, rows, cols, count), out_s...  43.8 us
    pallas_call x1, Pallas kernels, shards(): pl.pallas_call(put, out_shape=(jax.ShapeDtypeStruct((steps, rows, cols),...  1.57 us

profile of v1, /device:TPU:0, one launch (start us, length us, event | category | flops | bytes accessed | tf_op | source)
XLA Modules:
  0.0 46.0 jit_solution(6280003314441636623)
XLA Ops:
  0.6 43.8 %shard_map.59 = (f32[8,256,256]{2,1,0:T(8,128)S(1)}, f32[2,256,256]{2,1,0:T(8,128)S(1)}) custom-call(f32[8,256,256]{2,1,0:T(8,128)} %iterate_ref.1, f32[8,256,256]{2,1,0:T(8,128)} %source_ref.1, f32[256,256]{1,0:T(8,128)} %start_ref.1, f32[256,256]{1,0:T(8,128)} %conduct_ref.1), custom_call_target="tpu_custom_call" | custom-call | tf_op jit(solution)/shard_map/pallas_call | solution.py:631
  44.5 1.6 %shard_map.60 = (f32[8,256,256]{2,1,0:T(8,128)}, f32[2,256,256]{2,1,0:T(8,128)}) custom-call(f32[8,256,256]{2,1,0:T(8,128)S(1)} %get-tuple-element.4.a, f32[2,256,256]{2,1,0:T(8,128)S(1)} %get-tuple-element.5.b), custom_call_target="tpu_custom_call" | custom-call | tf_op jit(solution)/shard_map/pallas_call | solution.py:666
